TPU v7x, 32 devices: a 4x4x1 block of a 4x4x8 slice. The times are simulated.
32 devices in a mesh: pod: 1 (over z), dp: 4 (over y), tp: 8 (over x, core).
Axes of the slice: x: 4, y: 4, z: 1, core: 2. Of those that a mesh axis runs over, the one named last changes fastest.
The devices are a block of a 4x4x8 slice.
Arguments:
- x_saved: bfloat16 [6144, 4096], P(('pod', 'dp'))
- h_saved: bfloat16 [6144, 4096], P(('pod', 'dp'))
- mean_one: float32 [6144], P(('pod', 'dp'))
- rstd_one: float32 [6144], P(('pod', 'dp'))
- mean_two: float32 [6144], P(('pod', 'dp'))
- rstd_two: float32 [6144], P(('pod', 'dp'))
- gain_one: bfloat16 [4096], replicated
- gain_two: bfloat16 [4096], replicated
- grad_y: bfloat16 [6144, 4096], P(('pod', 'dp'))
- w_qkv: bfloat16 [4096, 3, 32, 128], P(None, None, 'tp')
- w_proj: bfloat16 [32, 128, 4096], P('tp')
- w_up: bfloat16 [4096, 16384], P(None, 'tp')
- w_down: bfloat16 [16384, 4096], P('tp')
Outputs:
- output 1: bfloat16 [6144, 4096], P(('pod', 'dp'))
- output 2: bfloat16 [4096, 3, 32, 128], P('pod', None, 'tp')
- output 3: bfloat16 [32, 128, 4096], P(('pod', 'tp'))
- output 4: bfloat16 [4096, 16384], P('pod', 'tp')
- output 5: bfloat16 [16384, 4096], P(('pod', 'tp'))
All inputs are finite; a program needn't handle non-finite values.
Results may differ from a plain program's by a relative error of at most 0.0192943.
Values are sent between devices in bfloat16 or wider.
A program may use at most 768 MiB of HBM per device.

v0:
```python
import math
import jax
import jax.numpy as jnp
from jax import lax
from jax.sharding import PartitionSpec as P

GELU_C = math.sqrt(2.0 / math.pi)


def layer_norm(row_vals, row_mean, row_rstd, gain_vec):
    x_hat = (row_vals.astype(jnp.float32) - row_mean[:, None]) * row_rstd[:, None]
    return x_hat, (x_hat * gain_vec.astype(jnp.float32)).astype(jnp.bfloat16)


def norm_back(d_norm, x_hat, row_rstd, gain_vec):
    scaled = d_norm * gain_vec.astype(jnp.float32)
    scaled_mean = jnp.mean(scaled, axis=-1, keepdims=True)
    proj_mean = jnp.mean(scaled * x_hat, axis=-1, keepdims=True)
    return row_rstd[:, None] * (scaled - scaled_mean - x_hat * proj_mean)


def gelu_pair(pre_act):
    pre_wide = pre_act.astype(jnp.float32)
    tanh_val = jnp.tanh(GELU_C * (pre_wide + 0.044715 * pre_wide * pre_wide * pre_wide))
    gelu_val = 0.5 * pre_wide * (1.0 + tanh_val)
    gelu_slope = 0.5 * (1.0 + tanh_val) + 0.5 * pre_wide * (1.0 - tanh_val * tanh_val) * GELU_C * (1.0 + 0.134145 * pre_wide * pre_wide)
    return gelu_val, gelu_slope


def causal_probs(q_heads, k_heads):
    tok_count = q_heads.shape[0]
    scores = jnp.einsum('qhe,khe->hqk', q_heads, k_heads, preferred_element_type=jnp.float32) * (q_heads.shape[-1] ** -0.5)
    row_ids = lax.broadcasted_iota(jnp.int32, (tok_count, tok_count), 0)
    col_ids = lax.broadcasted_iota(jnp.int32, (tok_count, tok_count), 1)
    scores = jnp.where(col_ids <= row_ids, scores, -1e30)
    shifted = jnp.exp(scores - jnp.max(scores, axis=-1, keepdims=True))
    return shifted / jnp.sum(shifted, axis=-1, keepdims=True)


def attn_grads(qkv_heads, prob_mat, prob_lo, d_attn):
    soft_scale = qkv_heads.shape[-1] ** -0.5
    dv_heads = jnp.einsum('hqk,qhe->khe', prob_lo, d_attn, preferred_element_type=jnp.float32).astype(jnp.bfloat16)
    d_probs = jnp.einsum('qhe,khe->hqk', d_attn, qkv_heads[:, 2], preferred_element_type=jnp.float32)
    d_scores = (prob_mat * (d_probs - jnp.sum(prob_mat * d_probs, axis=-1, keepdims=True)) * soft_scale).astype(jnp.bfloat16)
    dq_heads = jnp.einsum('hqk,khe->qhe', d_scores, qkv_heads[:, 1], preferred_element_type=jnp.float32).astype(jnp.bfloat16)
    dk_heads = jnp.einsum('hqk,qhe->khe', d_scores, qkv_heads[:, 0], preferred_element_type=jnp.float32).astype(jnp.bfloat16)
    return jnp.stack([dq_heads, dk_heads, dv_heads], axis=1)


def solution(mesh):
    row_spec = P(('pod', 'dp'), None)
    stat_spec = P(('pod', 'dp'))
    in_specs = (row_spec, row_spec, stat_spec, stat_spec, stat_spec, stat_spec, P(None), P(None), row_spec,
                P(None, None, 'tp', None), P('tp', None, None), P(None, 'tp'), P('tp', None))
    out_specs = (row_spec, P('pod', None, 'tp', None), P(('pod', 'tp'), None, None), P('pod', 'tp'), P(('pod', 'tp'), None))

    def local_step(x_saved, h_saved, mean_one, rstd_one, mean_two, rstd_two, gain_one, gain_two, grad_y, w_qkv, w_proj, w_up, w_down):
        hat_two, norm_two = layer_norm(h_saved, mean_two, rstd_two, gain_two)
        pre_act = jnp.dot(norm_two, w_up, preferred_element_type=jnp.float32).astype(jnp.bfloat16)
        gelu_val, gelu_slope = gelu_pair(pre_act)
        act_out = gelu_val.astype(jnp.bfloat16)
        d_act = lax.dot_general(grad_y, w_down, (((1,), (1,)), ((), ())), preferred_element_type=jnp.float32)
        d_pre = (d_act * gelu_slope).astype(jnp.bfloat16)
        grad_down = lax.dot_general(act_out, grad_y, (((0,), (0,)), ((), ())), preferred_element_type=jnp.float32)
        grad_up = lax.dot_general(norm_two, d_pre, (((0,), (0,)), ((), ())), preferred_element_type=jnp.float32)
        part_two = lax.dot_general(d_pre, w_up, (((1,), (1,)), ((), ())), preferred_element_type=jnp.float32).astype(jnp.bfloat16)
        d_norm_two = lax.psum(part_two, 'tp').astype(jnp.float32)
        d_mid = grad_y.astype(jnp.float32) + norm_back(d_norm_two, hat_two, rstd_two, gain_two)
        d_mid_lo = d_mid.astype(jnp.bfloat16)
        hat_one, norm_one = layer_norm(x_saved, mean_one, rstd_one, gain_one)
        qkv_heads = jnp.einsum('td,dche->tche', norm_one, w_qkv, preferred_element_type=jnp.float32).astype(jnp.bfloat16)
        prob_mat = causal_probs(qkv_heads[:, 0], qkv_heads[:, 1])
        prob_lo = prob_mat.astype(jnp.bfloat16)
        attn_out = jnp.einsum('hqk,khe->qhe', prob_lo, qkv_heads[:, 2], preferred_element_type=jnp.float32).astype(jnp.bfloat16)
        grad_proj = jnp.einsum('the,td->hed', attn_out, d_mid_lo, preferred_element_type=jnp.float32)
        d_attn = jnp.einsum('td,hed->the', d_mid_lo, w_proj, preferred_element_type=jnp.float32).astype(jnp.bfloat16)
        d_qkv = attn_grads(qkv_heads, prob_mat, prob_lo, d_attn)
        grad_qkv = jnp.einsum('td,tche->dche', norm_one, d_qkv, preferred_element_type=jnp.float32)
        part_one = jnp.einsum('tche,dche->td', d_qkv, w_qkv, preferred_element_type=jnp.float32).astype(jnp.bfloat16)
        d_norm_one = lax.psum(part_one, 'tp').astype(jnp.float32)
        grad_x = (d_mid + norm_back(d_norm_one, hat_one, rstd_one, gain_one)).astype(jnp.bfloat16)
        return (grad_x,
                lax.psum(grad_qkv, 'dp').astype(jnp.bfloat16),
                lax.psum(grad_proj, 'dp').astype(jnp.bfloat16),
                lax.psum(grad_up, 'dp').astype(jnp.bfloat16),
                lax.psum(grad_down, 'dp').astype(jnp.bfloat16))

    return jax.shard_map(local_step, mesh=mesh, in_specs=in_specs, out_specs=out_specs, check_vma=False)
```

profile of v0, /device:TPU:98, one launch (start us, length us, event | category | flops | bytes accessed | tf_op | source)
XLA Modules:
  0.0 2258.4 jit_solution(2696082136346539245)
XLA Ops:
  7.2 0.7 convert_element_type.103
  8.0 34.9 %convolution_convert_fusion.1 = bf16[1536,2048]{1,0:T(8,128)(2,1)} fusion(bf16[4096,2048]{1,0:T(8,128)(2,1)} %param.24, bf16[1536,4096]{1,0:T(8,128)(2,1)} %param.14, f32[4096]{0:T(1024)S(1)} %convert_element_type.103, f32[1536]{0:T(1024)} %param.17, f32[1536]{0:T(1024)} %param.18), kind=kOutput, calls=%fused_computation.60 | convolution fusion | flops 25804406784 | bytes 35680256 | tf_op jit(solution)/shard_map/dot_general | solution.py:59
  42.9 38.6 %fusion.25 = bf16[1536,2048]{1,0:T(8,128)(2,1)} fusion(bf16[1536,2048]{1,0:T(8,128)(2,1)} %convolution_convert_fusion.1, bf16[1536,4096]{1,0:T(8,128)(2,1)S(1)} %copy-done.2, bf16[2048,4096]{1,0:T(8,128)(2,1)} %param.25), kind=kOutput, calls=%fused_computation.42 | convolution fusion | flops 25832718336 | bytes 41943040 | tf_op jit(solution)/shard_map/dot_general | solution.py:62
  81.5 33.3 %convolution_convert_fusion = bf16[1536,4096]{1,0:T(8,128)(2,1)} fusion(bf16[1536,2048]{1,0:T(8,128)(2,1)} %fusion.25, bf16[4096,2048]{1,0:T(8,128)(2,1)} %param.24), kind=kOutput, calls=%fused_computation.35 | convolution fusion | flops 25776095232 | bytes 35651584 | tf_op jit(solution)/shard_map/dot_general | solution.py:66
  115.0 45.5 %fusion.42 = f32[2048,4096]{1,0:T(8,128)} fusion(bf16[1536,4096]{1,0:T(8,128)(2,1)} %param.21, bf16[1536,2048]{1,0:T(8,128)(2,1)} %convolution_convert_fusion.1), kind=kOutput, calls=%fused_computation.61 | convolution fusion | flops 25801261056 | bytes 52428800 | tf_op jit(solution)/shard_map/dot_general | solution.py:64
  160.6 27.4 %fusion.53 = bf16[1536,3,4,128]{3,0,2,1:T(8,128)(2,1)} fusion(bf16[4096,3,4,128]{3,2,1,0:T(4,128)(2,1)} %param.22, bf16[1536,4096]{1,0:T(8,128)(2,1)} %param.13, f32[4096]{0:T(1024)S(1)} %convert_element_type.111, f32[1536]{0:T(1024)S(1)} %copy-done.9, f32[1536]{0:T(1024)S(1)} %copy-done.11), kind=kOutput, calls=%fused_computation.70 | convolution fusion | flops 19361169408 | bytes 29913088 | tf_op jit(solution)/shard_map/td,dche->tche/dot_general | solution.py:71
  188.0 41.5 %fusion.101 = f32[4096,2048]{1,0:T(8,128)} fusion(bf16[1536,2048]{1,0:T(8,128)(2,1)} %fusion.25, bf16[1536,4096]{1,0:T(8,128)(2,1)S(1)} %bitcast.70, f32[4096]{0:T(1024)S(1)} %copy-done.6, f32[1536]{0:T(1024)S(1)} %copy-done.7, f32[1536]{0:T(1024)S(1)} %copy-done.8), kind=kOutput, calls=%fused_computation.101 | convolution fusion | flops 25801261056 | bytes 52457472 | tf_op jit(solution)/shard_map/dot_general | solution.py:65
  229.5 0.7 iota_compare_fusion
  230.2 21.4 exponential_reduce_fusion
  251.6 2.5 all-reduce.5.cloned.1.call-done
  254.2 12.8 fusion.12
  267.0 23.4 %multiply_add_fusion = f32[1536,4096]{1,0:T(8,128)} fusion(bf16[1536,4096]{1,0:T(8,128)(2,1)S(1)} %copy-done, bf16[1536,4096]{1,0:T(8,128)(2,1)} %param.14, bf16[1536,4096]{1,0:T(8,128)(2,1)} %param.21, f32[1536]{0:T(1024)S(1)} %get-tuple-element.20, f32[1536]{0:T(1024)S(1)} %get-tuple-element.21, f32[4096]{0:T(1024)S(1)} %copy-done.6, ...), kind=kLoop, calls=%fused_computation.27 | loop fusion | flops 69206016 | bytes 62955520 | tf_op jit(solution)/shard_map/add | solution.py:68
  290.4 11.7 fusion.58
  302.1 27.9 %fusion.31 = f32[4,128,4096]{2,1,0:T(8,128)} fusion(f32[1536,4096]{1,0:T(8,128)} %multiply_add_fusion, bf16[1536,3,4,128]{3,0,2,1:T(8,128)(2,1)} %fusion.53, f32[4,1536,1536]{1,2,0:T(8,128)} %get-tuple-element.19, f32[4,1536]{1,0:T(4,128)S(1)} %get-tuple-element.18), kind=kOutput, calls=%fused_computation.48 | convolution fusion | flops 8884322304 | bytes 72900608 | tf_op jit(solution)/shard_map/the,td->hed/dot_general | solution.py:75
  329.9 14.4 fusion.78
  344.3 16.2 fusion.87
  360.5 49.1 %fusion.84 = bf16[1536,1,4,128]{0,3,2,1:T(8,128)(2,1)} fusion(f32[4,1536,1536]{1,2,0:T(8,128)} %fusion.87, bf16[1536,3,4,128]{3,0,2,1:T(8,128)(2,1)} %fusion.53, f32[4,1536,1536]{1,2,0:T(8,128)} %get-tuple-element.19, f32[4,1536]{1,0:T(4,128)S(1)} %get-tuple-element.18), kind=kOutput, calls=%fused_computation.79 | convolution fusion | flops 2482773504 | bytes 154189824 | tf_op jit(solution)/shard_map/hqk,khe->qhe/dot_general | solution.py:45
  409.6 50.0 %fusion.81 = bf16[1536,1,4,128]{0,3,2,1:T(8,128)(2,1)} fusion(f32[4,1536,1536]{1,2,0:T(8,128)} %fusion.87, bf16[1536,3,4,128]{3,0,2,1:T(8,128)(2,1)} %fusion.53, f32[4,1536,1536]{1,2,0:T(8,128)} %get-tuple-element.19, f32[4,1536]{1,0:T(4,128)S(1)} %get-tuple-element.18), kind=kOutput, calls=%fused_computation.78 | convolution fusion | flops 2482773504 | bytes 154189824 | tf_op jit(solution)/shard_map/hqk,qhe->khe/dot_general | solution.py:46
  459.6 25.1 %bitcast_convert_fusion = bf16[1536,4096]{1,0:T(8,128)(2,1)} fusion(bf16[4096,3,4,128]{3,2,1,0:T(4,128)(2,1)} %param.22, bf16[1536,1,4,128]{0,3,2,1:T(8,128)(2,1)S(1)} %fusion.78, bf16[1536,1,4,128]{0,3,2,1:T(8,128)(2,1)} %fusion.81, bf16[1536,1,4,128]{0,3,2,1:T(8,128)(2,1)} %fusion.84), kind=kOutput, calls=%fused_computation.20 | convolution fusion | flops 19338362880 | bytes 29884416 | tf_op jit(solution)/shard_map/tche,dche->td/dot_general | solution.py:79
  484.8 27.8 %fusion.50 = f32[4096,3,4,128]{3,0,2,1:T(8,128)} fusion(bf16[1536,4096]{1,0:T(8,128)(2,1)} %param.13, f32[4096]{0:T(1024)S(1)} %copy-done.4, f32[1536]{0:T(1024)S(1)} %copy-done.10, f32[1536]{0:T(1024)S(1)} %copy-done.12, bf16[1536,1,4,128]{0,3,2,1:T(8,128)(2,1)S(1)} %fusion.78, bf16[1536,1,4,128]{0,3,2,1:T(8,128)(2,1)} %fusion.81, ...), kind=kOutput, calls=%fused_computation.68 | convolution fusion | flops 19372965888 | bytes 42496000 | tf_op jit(solution)/shard_map/td,tche->dche/dot_general | solution.py:78
  512.6 1687.0 %all-reduce.8 = (bf16[4096,3,4,128]{3,0,2,1:T(8,128)(2,1)}, bf16[4,128,4096]{2,1,0:T(8,128)(2,1)}, bf16[4096,2048]{1,0:T(8,128)(2,1)}, bf16[2048,4096]{1,0:T(8,128)(2,1)}) all-reduce(f32[4096,3,4,128]{3,0,2,1:T(8,128)} %fusion.50, f32[4,128,4096]{2,1,0:T(8,128)} %fusion.31, ...), channel_id=1, replica_groups=mesh['pod'=1,'dp'=4,'tp'=8] {'dp'}, use_global_device_ids=true, to_apply=%region_9.10 | all-reduce | flops 25165824 | bytes 150994944 | tf_op jit(solution)/shard_map/psum | solution.py:83
  2199.6 17.1 copy.29
  2216.8 12.8 fusion.11
  2229.6 21.5 add_convert_fusion
  (46 shorter events, 0.3 us)
Async XLA Ops:
  7.2 247.0 %all-reduce.5.cloned.1.call-start = ((), (), s32[]{:S(2)}) async-start(), calls=%async_computation | async-start | bytes 25165824 | tf_op jit(solution)/shard_map/psum | solution.py:67
  7.9 35.0 %copy-start.5 = (f32[4096]{0:T(1024)}, f32[4096]{0:T(1024)S(1)}, u32[]{:S(2)}) copy-start(f32[4096]{0:T(1024)S(1)} %convert_element_type.103) | copy-start | bytes 49156
  7.9 35.0 %copy-start.2 = (bf16[1536,4096]{1,0:T(8,128)(2,1)S(1)}, bf16[1536,4096]{1,0:T(8,128)(2,1)}, u32[]{:S(2)}) copy-start(bf16[1536,4096]{1,0:T(8,128)(2,1)} %param.21) | copy-start | bytes 37748740
  114.8 45.7 %copy-start.13 = (bf16[4096]{0:T(1024)(128)(2,1)S(1)}, bf16[4096]{0:T(1024)(128)(2,1)}, u32[]{:S(2)}) copy-start(bf16[4096]{0:T(1024)(128)(2,1)} %param.19) | copy-start | bytes 24580
  114.9 45.7 %copy-start.9 = (f32[1536]{0:T(1024)S(1)}, f32[1536]{0:T(1024)}, u32[]{:S(2)}) copy-start(f32[1536]{0:T(1024)} %param.15) | copy-start | bytes 18436
  114.9 45.6 %copy-start.11 = (f32[1536]{0:T(1024)S(1)}, f32[1536]{0:T(1024)}, u32[]{:S(2)}) copy-start(f32[1536]{0:T(1024)} %param.16) | copy-start | bytes 18436
  114.9 2101.9 %all-reduce.7.cloned.1.call-start = ((), (), s32[]{:S(2)}) async-start(), calls=%async_computation.1 | async-start | bytes 25165824 | tf_op jit(solution)/shard_map/psum | solution.py:80
  115.0 73.0 %slice-start = ((s8[12582912]{0:T(1024)(128)(4,1)}), s8[4194304]{0:T(1024)(128)(4,1)S(1)}, s32[]{:S(2)}) async-start(s8[12582912]{0:T(1024)(128)(4,1)} %bitcast.69), calls=%async_computation.2 | async-start | bytes 8388608
  115.0 73.0 %slice-start.1 = ((s8[12582912]{0:T(1024)(128)(4,1)}), s8[4194304]{0:T(1024)(128)(4,1)S(1)}, s32[]{:S(2)}) async-start(s8[12582912]{0:T(1024)(128)(4,1)} %bitcast.69), calls=%async_computation.3 | async-start | bytes 8388608
  160.5 27.5 %copy-start.3 = (f32[4096]{0:T(1024)}, f32[4096]{0:T(1024)S(1)}, u32[]{:S(2)}) copy-start(f32[4096]{0:T(1024)S(1)} %convert_element_type.111) | copy-start | bytes 49156
  160.5 27.5 %slice-start.2 = ((s8[12582912]{0:T(1024)(128)(4,1)}), s8[4194304]{0:T(1024)(128)(4,1)S(1)}, s32[]{:S(2)}) async-start(s8[12582912]{0:T(1024)(128)(4,1)} %bitcast.69), calls=%async_computation.4 | async-start | bytes 8388608
  160.5 27.5 %copy-start.6 = (f32[4096]{0:T(1024)S(1)}, f32[4096]{0:T(1024)}, u32[]{:S(2)}) copy-start(f32[4096]{0:T(1024)} %copy-done.5) | copy-start | bytes 49156
  160.6 27.5 %copy-start.7 = (f32[1536]{0:T(1024)S(1)}, f32[1536]{0:T(1024)}, u32[]{:S(2)}) copy-start(f32[1536]{0:T(1024)} %param.17) | copy-start | bytes 18436
  160.6 27.5 %copy-start.8 = (f32[1536]{0:T(1024)S(1)}, f32[1536]{0:T(1024)}, u32[]{:S(2)}) copy-start(f32[1536]{0:T(1024)} %param.18) | copy-start | bytes 18436
  254.2 12.8 copy-start
  267.0 23.4 %copy-start.14 = (bf16[4,128,4096]{2,1,0:T(8,128)(2,1)S(1)}, bf16[4,128,4096]{2,1,0:T(8,128)(2,1)}, u32[]{:S(2)}) copy-start(bf16[4,128,4096]{2,1,0:T(8,128)(2,1)} %param.23) | copy-start | bytes 12582916
  459.6 25.1 %copy-start.4 = (f32[4096]{0:T(1024)S(1)}, f32[4096]{0:T(1024)}, u32[]{:S(2)}) copy-start(f32[4096]{0:T(1024)} %copy-done.3) | copy-start | bytes 49156
  459.6 25.1 %copy-start.10 = (f32[1536]{0:T(1024)S(1)}, f32[1536]{0:T(1024)}, u32[]{:S(2)}) copy-start(f32[1536]{0:T(1024)} %param.15) | copy-start | bytes 18436
  459.6 25.1 %copy-start.12 = (f32[1536]{0:T(1024)S(1)}, f32[1536]{0:T(1024)}, u32[]{:S(2)}) copy-start(f32[1536]{0:T(1024)} %param.16) | copy-start | bytes 18436
  2216.8 12.8 copy-start.1
Sparse Core Ops, SparseCore 0:
  115.0 139.1 all-reduce.4
  512.7 138.6 all-reduce.6
where the time goes:
time: 2260 us
  blocking collectives  1690 us (75%)
  matrix products  465 us (21%)
  other arithmetic  71.9 us (3%)
    psum x1, blocking collectives, local_step(): lax.psum(grad_qkv, 'dp').astype(jnp.bfloat16)  1690 us
    dot_general x1, matrix products, attn_grads(): jnp.einsum('hqk,qhe->khe', d_scores, qkv_heads[:, 0], preferred_element_t...  50 us
    dot_general x1, matrix products, attn_grads(): jnp.einsum('hqk,khe->qhe', d_scores, qkv_heads[:, 1], preferred_element_t...  49.1 us
    dot_general x1, matrix products, local_step(): lax.dot_general(act_out, grad_y, (((0,), (0,)), ((), ())), preferred_elem...  45.5 us
  transfers between devices with their start and end apart: 2, of which 1 were waited for; matrix products, arithmetic and copies ran while one was open for 7% of the time, Pallas kernels for 0%

commit v1 on v0

v1 whole, which is shorter than its diff:
```python
import functools
import math
import jax
import jax.numpy as jnp
from jax import lax
from jax.experimental import pallas as pl
from jax.experimental.pallas import tpu as pltpu
from jax.sharding import PartitionSpec as P

GELU_C = math.sqrt(2.0 / math.pi)
VMEM_BYTES = 60 * 1024 * 1024
F32 = jnp.float32
BF16 = jnp.bfloat16


def layer_norm(row_vals, row_mean, row_rstd, gain_vec):
    x_hat = (row_vals.astype(F32) - row_mean[:, None]) * row_rstd[:, None]
    return x_hat, (x_hat * gain_vec.astype(F32)).astype(BF16)


def norm_back(d_norm, x_hat, row_rstd, gain_vec):
    scaled = d_norm * gain_vec.astype(F32)
    scaled_mean = jnp.mean(scaled, axis=-1, keepdims=True)
    proj_mean = jnp.mean(scaled * x_hat, axis=-1, keepdims=True)
    return row_rstd[:, None] * (scaled - scaled_mean - x_hat * proj_mean)


def gelu_pair(pre_wide):
    square = pre_wide * pre_wide
    half_up = 0.5 + 0.5 * jnp.tanh(pre_wide * (GELU_C + (GELU_C * 0.044715) * square))
    gelu_val = pre_wide * half_up
    gelu_slope = half_up + gelu_val * (1.0 - half_up) * (2.0 * GELU_C + (2.0 * GELU_C * 0.134145) * square)
    return gelu_val, gelu_slope


def hold(*values):
    return lax.optimization_barrier(values)


def tile_of(size, want):
    return want if size % want == 0 else size


def up_proj(first_block, norm_rows, w_up, row_count, row_tile):
    total, depth = norm_rows.shape
    cols = w_up.shape[1]
    col_tile = tile_of(cols, 1024)
    blocks = total // row_tile

    def body(first, n_ref, w_ref, out_ref):
        out_ref[...] = jnp.dot(n_ref[...], w_ref[...], preferred_element_type=F32).astype(BF16)

    return pl.pallas_call(
        body,
        out_shape=jax.ShapeDtypeStruct((row_count, cols), BF16),
        grid_spec=pltpu.PrefetchScalarGridSpec(
            num_scalar_prefetch=1, grid=(row_count // row_tile, cols // col_tile),
            in_specs=[pl.BlockSpec((row_tile, depth), lambda i, j, first: (lax.rem(first[0] + i, blocks), 0)),
                      pl.BlockSpec((depth, col_tile), lambda i, j, first: (0, j))],
            out_specs=pl.BlockSpec((row_tile, col_tile), lambda i, j, first: (i, j))),
        compiler_params=pltpu.CompilerParams(vmem_limit_bytes=VMEM_BYTES),
        cost_estimate=pl.CostEstimate(flops=2 * row_count * depth * cols, transcendentals=0,
                                      bytes_accessed=2 * (row_count * (depth + cols) + depth * cols)),
        name="up_proj",
    )(first_block, norm_rows, w_up)


def down_back(first_block, grad_rows, w_down, pre_act, row_tile, total, prior=None):
    row_count, cols = pre_act.shape
    depth = grad_rows.shape[1]
    col_tile = tile_of(cols, 512)
    out_blocks = total // row_tile
    local = prior is None

    def body(first, d_ref, w_ref, a_ref, *rest):
        outs = rest if local else rest[2:]
        sub = tile_of(col_tile, 256)
        for at in range(0, col_tile, sub):
            d_act = lax.dot_general(d_ref[...], w_ref[at:at + sub, :], (((1,), (1,)), ((), ())), preferred_element_type=F32)
            gelu_val, gelu_slope = gelu_pair(a_ref[:, at:at + sub].astype(F32))
            d_pre = (d_act * gelu_slope).astype(BF16)
            outs[0][:, at:at + sub] = gelu_val.astype(BF16)
            outs[1][:, at:at + sub] = d_pre
            if local:
                outs[2][:, at:at + sub] = d_pre

    wrap = lambda i, j, first: (lax.rem(first[0] + i, out_blocks), j)
    in_rows = (lambda i, j, first: (i, 0)) if local else (lambda i, j, first: (lax.rem(first[0] + i, out_blocks), 0))
    in_specs = [pl.BlockSpec((row_tile, depth), in_rows),
                pl.BlockSpec((col_tile, depth), lambda i, j, first: (j, 0)),
                pl.BlockSpec((row_tile, col_tile), lambda i, j, first: (i, j))]
    out_specs = [pl.BlockSpec((row_tile, col_tile), wrap)] * 2
    out_shape = [jax.ShapeDtypeStruct((total, cols), BF16)] * 2
    args = [first_block, grad_rows, w_down, pre_act]
    aliases = {}
    if local:
        out_specs = out_specs + [pl.BlockSpec((row_tile, col_tile), lambda i, j, first: (i, j))]
        out_shape = out_shape + [jax.ShapeDtypeStruct((row_count, cols), BF16)]
    else:
        in_specs = in_specs + [pl.BlockSpec(memory_space=pl.ANY)] * 2
        args = args + list(prior)
        aliases = {4: 0, 5: 1}
    return pl.pallas_call(
        body,
        out_shape=out_shape,
        grid_spec=pltpu.PrefetchScalarGridSpec(
            num_scalar_prefetch=1, grid=(row_count // row_tile, cols // col_tile),
            in_specs=in_specs, out_specs=out_specs),
        input_output_aliases=aliases,
        compiler_params=pltpu.CompilerParams(vmem_limit_bytes=VMEM_BYTES),
        cost_estimate=pl.CostEstimate(flops=2 * row_count * depth * cols, transcendentals=row_count * cols,
                                      bytes_accessed=2 * (row_count * (depth + 3 * cols) + depth * cols)),
        name="down_back",
    )(*args)


def attention_back(qkv, d_attn):
    _, heads, toks, size = qkv.shape
    q_tile = tile_of(toks, 512)
    steps = toks // q_tile
    scale = size ** -0.5

    def dot(a, b, ca, cb):
        return lax.dot_general(a, b, (((ca,), (cb,)), ((), ())), preferred_element_type=F32)

    def body(q_ref, k_ref, v_ref, do_ref, o_ref, g_ref, dk_acc, dv_acc):
        step = pl.program_id(1)

        @pl.when(step == 0)
        def _():
            dk_acc[...] = jnp.zeros_like(dk_acc)
            dv_acc[...] = jnp.zeros_like(dv_acc)

        def block(n):
            seen = (n + 1) * q_tile
            q, d_out = q_ref[0, 0], do_ref[0]
            k, v = k_ref[0, 0, :seen, :], v_ref[0, 0, :seen, :]
            scores = dot(q, k, 1, 1) * scale
            rows = lax.broadcasted_iota(jnp.int32, (q_tile, seen), 0) + n * q_tile
            cols = lax.broadcasted_iota(jnp.int32, (q_tile, seen), 1)
            scores = jnp.where(cols <= rows, scores, -1e30)
            shifted = jnp.exp(scores - jnp.max(scores, axis=-1, keepdims=True))
            probs = shifted * (1.0 / jnp.sum(shifted, axis=-1, keepdims=True))
            probs_lo = probs.astype(BF16)
            o_ref[0] = dot(probs_lo, v, 1, 0).astype(BF16)
            dv_acc[:seen, :] += dot(probs_lo, d_out, 0, 0)
            d_probs = dot(d_out, v, 1, 1)
            inner = jnp.sum(probs * d_probs, axis=-1, keepdims=True)
            d_scores = (probs * (d_probs - inner) * scale).astype(BF16)
            g_ref[0, 0, n * q_tile:seen, :] = dot(d_scores, k, 1, 0).astype(BF16)
            dk_acc[:seen, :] += dot(d_scores, q, 0, 0)

        for n in range(steps):
            pl.when(step == n)(functools.partial(block, n))

        @pl.when(step == steps - 1)
        def _():
            g_ref[1, 0] = dk_acc[...].astype(BF16)
            g_ref[2, 0] = dv_acc[...].astype(BF16)

    return pl.pallas_call(
        body,
        out_shape=[jax.ShapeDtypeStruct((heads, toks, size), BF16), jax.ShapeDtypeStruct(qkv.shape, BF16)],
        grid=(heads, steps),
        in_specs=[pl.BlockSpec((1, 1, q_tile, size), lambda h, i: (0, h, i, 0)),
                  pl.BlockSpec((1, 1, toks, size), lambda h, i: (1, h, 0, 0)),
                  pl.BlockSpec((1, 1, toks, size), lambda h, i: (2, h, 0, 0)),
                  pl.BlockSpec((1, q_tile, size), lambda h, i: (h, i, 0))],
        out_specs=[pl.BlockSpec((1, q_tile, size), lambda h, i: (h, i, 0)),
                   pl.BlockSpec((3, 1, toks, size), lambda h, i: (0, h, 0, 0))],
        scratch_shapes=[pltpu.VMEM((toks, size), F32), pltpu.VMEM((toks, size), F32)],
        compiler_params=pltpu.CompilerParams(vmem_limit_bytes=VMEM_BYTES),
        cost_estimate=pl.CostEstimate(flops=40 * heads * toks * toks * size, transcendentals=heads * toks * toks,
                                      bytes_accessed=2 * 8 * heads * toks * size),
        name="attention_back",
    )(qkv, qkv, qkv, d_attn)


def solution(mesh):
    row_spec = P(('pod', 'dp'), None)
    stat_spec = P(('pod', 'dp'))
    in_specs = (row_spec, row_spec, stat_spec, stat_spec, stat_spec, stat_spec, P(None), P(None), row_spec,
                P(None, None, 'tp', None), P('tp', None, None), P(None, 'tp'), P('tp', None))
    out_specs = (row_spec, P('pod', None, 'tp', None), P(('pod', 'tp'), None, None), P('pod', 'tp'), P(('pod', 'tp'), None))
    tp_ways, dp_ways = mesh.shape['tp'], mesh.shape['dp']

    def layer_step(x_saved, h_saved, mean_one, rstd_one, mean_two, rstd_two, gain_one, gain_two, grad_y, w_qkv, w_proj, w_up, w_down):
        toks, width = x_saved.shape
        share = toks // tp_ways
        total = toks * dp_ways
        tp_at, dp_at = lax.axis_index('tp'), lax.axis_index('dp')
        mine = lambda a: lax.dynamic_slice_in_dim(a, tp_at * share, share, 0)
        row_tile = tile_of(toks, 512)
        seq_blocks = toks // row_tile
        later = lambda n: ((dp_at + n) * seq_blocks).astype(jnp.int32).reshape(1)
        zero_block = jnp.zeros((1,), jnp.int32)

        dy_mine = mine(grad_y)
        hat_two, norm_two_mine = layer_norm(mine(h_saved), mine(mean_two), mine(rstd_two), gain_two)
        norm_two_all = lax.all_gather(norm_two_mine, ('dp', 'tp'), tiled=True)

        _, norm_two = layer_norm(h_saved, mean_two, rstd_two, gain_two)
        pre_own = up_proj(zero_block, norm_two, w_up, toks, row_tile)
        act_all, d_pre_all, d_pre_own = down_back(later(0), grad_y, w_down, pre_own, row_tile, total)
        part_two = lax.dot_general(d_pre_own, w_up, (((1,), (1,)), ((), ())), preferred_element_type=F32).astype(BF16)
        d_norm_two = lax.psum_scatter(part_two, 'tp', scatter_dimension=0, tiled=True)

        _, norm_one = layer_norm(x_saved, mean_one, rstd_one, gain_one)
        qkv = jnp.einsum('td,dche->chte', norm_one, w_qkv, preferred_element_type=F32).astype(BF16)
        norm_two_all, qkv = hold(norm_two_all, qkv)
        pre_next = up_proj(later(1), norm_two_all, w_up, toks, row_tile)

        d_norm_two, pre_next, dy_mine = hold(d_norm_two, pre_next, dy_mine)
        d_mid = dy_mine.astype(F32) + norm_back(d_norm_two.astype(F32), hat_two, mine(rstd_two), gain_two)
        d_mid_mine, norm_two_all, dy_mine = hold(d_mid.astype(BF16), norm_two_all, dy_mine)
        d_mid_lo = lax.all_gather(d_mid_mine, 'tp', tiled=True)
        dy_all = lax.all_gather(dy_mine, ('dp', 'tp'), tiled=True)
        pre_rest = up_proj(later(2), norm_two_all, w_up, total - 2 * toks, row_tile)

        d_mid_lo, pre_rest = hold(d_mid_lo, pre_rest)
        d_attn = jnp.einsum('td,hed->hte', d_mid_lo, w_proj, preferred_element_type=F32).astype(BF16)
        attn_out, d_qkv = attention_back(qkv, d_attn)

        sum_proj = jnp.einsum('hte,td->hed', attn_out, d_mid_lo, preferred_element_type=F32).reshape(-1, width)
        sum_qkv = jnp.einsum('chte,td->ched', d_qkv, norm_one, preferred_element_type=F32).reshape(-1, width)
        sum_proj = lax.psum_scatter(sum_proj, 'dp', scatter_dimension=0, tiled=True)
        sum_qkv = lax.psum_scatter(sum_qkv, 'dp', scatter_dimension=0, tiled=True)

        part_one = jnp.einsum('chte,dche->td', d_qkv, w_qkv, preferred_element_type=F32).astype(BF16)
        parts_one = lax.all_to_all(part_one.reshape(tp_ways, share, width), 'tp', 0, 0)

        act_all, d_pre_all = down_back(later(1), dy_all, w_down, pre_next, row_tile, total, (act_all, d_pre_all))
        d_pre_all, parts_one = hold(d_pre_all, parts_one)
        d_norm_one = jnp.sum(parts_one.astype(F32), axis=0)
        hat_one, _ = layer_norm(mine(x_saved), mine(mean_one), mine(rstd_one), gain_one)
        grad_x_mine = (d_mid + norm_back(d_norm_one, hat_one, mine(rstd_one), gain_one)).astype(BF16)
        pre_rest, grad_x_mine = hold(pre_rest, grad_x_mine)
        moved = [lax.ppermute(grad_x_mine, 'tp', [(i, (i + n) % tp_ways) for i in range(tp_ways)]) for n in range(1, tp_ways)]
        act_all, d_pre_all = down_back(later(2), dy_all, w_down, pre_rest, row_tile, total, (act_all, d_pre_all))
        d_pre_all, sum_proj = hold(d_pre_all, sum_proj)
        proj_piece = sum_proj.astype(BF16)
        act_all, proj_piece = hold(act_all, proj_piece)
        grad_proj = lax.all_gather(proj_piece, 'dp', tiled=True).reshape(w_proj.shape)
        grad_down = lax.dot_general(act_all, dy_all, (((0,), (0,)), ((), ())), preferred_element_type=F32).astype(BF16)

        grad_down, sum_qkv, *moved = hold(grad_down, sum_qkv, *moved)
        grad_x = jnp.zeros(x_saved.shape, BF16)
        for n, rows in enumerate([grad_x_mine] + moved):
            grad_x = lax.dynamic_update_slice_in_dim(grad_x, rows, lax.rem(tp_at + tp_ways - n, tp_ways) * share, 0)
        qkv_piece = jnp.swapaxes(sum_qkv.astype(BF16).reshape(-1, qkv.shape[3], width), 1, 2).reshape(-1, qkv.shape[3])
        norm_two_all, qkv_piece = hold(norm_two_all, qkv_piece)
        grad_qkv = lax.all_gather(qkv_piece, 'dp', tiled=True)
        grad_qkv = jnp.moveaxis(grad_qkv.reshape(qkv.shape[:2] + (width, qkv.shape[3])), 2, 0)
        grad_up = lax.dot_general(norm_two_all, d_pre_all, (((0,), (0,)), ((), ())), preferred_element_type=F32).astype(BF16)
        return grad_x, grad_qkv, grad_proj, grad_up, grad_down

    return jax.shard_map(layer_step, mesh=mesh, in_specs=in_specs, out_specs=out_specs, check_vma=False)
```

time: 2260 us -> 998 us (0.44)
  blocking collectives: 1690 us -> 0 us
  Pallas kernels: 0 us -> 336 us
  waiting for transfers between devices: 2.65 us -> 142 us
  matrix products: 465 us -> 377 us
  local copies, waits for them, and re-layouts: 17.2 us -> 54.4 us
  other arithmetic: 71.9 us -> 45.4 us
    psum x1 -> x0, blocking collectives: 1690 us -> none  [local_step(): lax.psum(grad_qkv, 'dp').astype(jnp.bfloat16)]
    pallas_call x0 -> x7, Pallas kernels: none -> 336 us  [the longest x3 168 us: down_back(): pl.pallas_call(body, out_shape=out_shape, grid_spec=pltpu.PrefetchScalarG...]
    all_gather x0 -> x5, waiting for transfers between devices: none -> 74.2 us  [the longest x1 73.9 us: layer_step(): dy_all = lax.all_gather(dy_mine, ('dp', 'tp'), tiled=True)]
    dot_general x14 -> x8, matrix products: 443 us -> 377 us  [the longest x1 118 us: layer_step(): lax.dot_general(norm_two_all, d_pre_all, (((0,), (0,)), ((), ())), prefer...]
    all_to_all x0 -> x1, waiting for transfers between devices: none -> 47.9 us  [layer_step(): lax.all_to_all(part_one.reshape(tp_ways, share, width), 'tp', 0, 0)]
    add x1 -> x0, other arithmetic: 23.4 us -> none  [local_step(): grad_y.astype(jnp.float32)]
  transfers between devices with their start and end apart: 2 -> 16, of which waited for: 1 -> 4; matrix products, arithmetic and copies ran while one was open for 7% -> 45% of each run, Pallas kernels for 0% -> 34%
where the time goes in v1:
time: 998 us; the launch traced here: 986 us
  matrix products  377 us (38%)
  Pallas kernels  336 us (34%)
  waiting for transfers between devices  142 us (14%)
  local copies, waits for them, and re-layouts  54.4 us (5%)
  other arithmetic  45.4 us (5%)
  between operations  16.2 us (2%)
  starting transfers between devices  15.3 us (2%)
    pallas_call x3, Pallas kernels, down_back(): pl.pallas_call(body, out_shape=out_shape, grid_spec=pltpu.PrefetchScalarG...  168 us
    pallas_call x3, Pallas kernels, up_proj(): pl.pallas_call(body, out_shape=jax.ShapeDtypeStruct((row_count, cols), BF...  133 us
    dot_general x1, matrix products, layer_step(): lax.dot_general(norm_two_all, d_pre_all, (((0,), (0,)), ((), ())), prefer...  118 us
    dot_general x1, matrix products, layer_step(): lax.dot_general(act_all, dy_all, (((0,), (0,)), ((), ())), preferred_elem...  118 us
    all_gather x1, waiting for transfers between devices, layer_step(): dy_all = lax.all_gather(dy_mine, ('dp', 'tp'), tiled=True)  73.9 us
    all_to_all x1, waiting for transfers between devices, layer_step(): lax.all_to_all(part_one.reshape(tp_ways, share, width), 'tp', 0, 0)  47.9 us
    pallas_call x1, Pallas kernels, attention_back(): pl.pallas_call(body, out_shape=[jax.ShapeDtypeStruct((heads, toks, size),...  34.7 us
    dot_general x1, matrix products, layer_step(): lax.dot_general(d_pre_own, w_up, (((1,), (1,)), ((), ())), preferred_elem...  33.6 us
  transfers between devices with their start and end apart: 16, of which 4 were waited for; matrix products, arithmetic and copies ran while one was open for 45% of the time, Pallas kernels for 34%

profile of v1, /device:TPU:98, one launch (start us, length us, event | category | flops | bytes accessed | tf_op | source)
XLA Modules:
  0.0 985.7 jit_solution(13466288776412379516)
XLA Ops:
  13.7 12.9 %multiply_convert_fusion.1.n_ref = bf16[1536,4096]{1,0:T(8,128)(2,1)} fusion(bf16[1536,4096]{1,0:T(8,128)(2,1)} %param.14, f32[4096]{0:T(1024)S(1)} %convert_element_type.75, f32[1536]{0:T(1024)} %param.18, f32[1536]{0:T(1024)} %param.17), kind=kLoop, calls=%fused_computation.3 | loop fusion | flops 31457280 | bytes 25194496 | tf_op jit(solution)/shard_map/convert_element_type | solution.py:18
  26.6 34.4 %up_proj.3.a_ref = bf16[1536,2048]{1,0:T(8,128)(2,1)} custom-call(s32[1]{0:T(128)} %constant.58.clone.1.first, bf16[1536,4096]{1,0:T(8,128)(2,1)} %multiply_convert_fusion.1.n_ref, bf16[4096,2048]{1,0:T(8,128)(2,1)} %w_ref.9), custom_call_target="tpu_custom_call" | custom-call | flops 25769803776 | bytes 35651584 | tf_op jit(solution)/shard_map/up_proj/pallas_call | solution.py:53
  61.0 45.1 %down_back.3 = (bf16[6144,2048]{1,0:T(8,128)(2,1)}, bf16[6144,2048]{1,0:T(8,128)(2,1)}, bf16[1536,2048]{1,0:T(8,128)(2,1)}) custom-call(s32[1]{0:T(128)} %bitcast.first, bf16[1536,4096]{1,0:T(8,128)(2,1)} %d_ref.1, bf16[2048,4096]{1,0:T(8,128)(2,1)} %w_ref.11, bf16[1536,2048]{1,0:T(8,128)(2,1)} %up_proj.3.a_ref), custom_call_target="tpu_custom_call" | custom-call | flops 25769803776 | bytes 48234496 | tf_op jit(solution)/shard_map/down_back/pallas_call | solution.py:103
  106.1 33.6 %convolution_convert_fusion.2 = bf16[1536,4096]{1,0:T(8,128)(2,1)} fusion(bf16[1536,2048]{1,0:T(8,128)(2,1)} %get-tuple-element.43, bf16[4096,2048]{1,0:T(8,128)(2,1)} %w_ref.9), kind=kOutput, calls=%fused_computation.6 | convolution fusion | flops 25776095232 | bytes 35651584 | tf_op jit(solution)/shard_map/dot_general | solution.py:205
  142.3 28.0 %convert_bitcast_fusion.q_ref.k_ref.v_ref = bf16[3,4,1536,128]{3,2,1,0:T(8,128)(2,1)} fusion(bf16[4096,3,4,128]{3,2,1,0:T(4,128)(2,1)} %param.22, bf16[1536,4096]{1,0:T(8,128)(2,1)} %param.13, f32[4096]{0:T(1024)S(1)} %convert_element_type.81, f32[1536]{0:T(1024)S(1)} %copy-done.21, f32[1536]{0:T(1024)S(1)} %copy-done.23), kind=kOutput, calls=%fused_computation.16 | convolution fusion | flops 19361169408 | bytes 29913088 | tf_op jit(solution)/shard_map/td,dche->chte/dot_general | solution.py:209
  170.3 34.4 %up_proj.4.a_ref = bf16[1536,2048]{1,0:T(8,128)(2,1)} custom-call(s32[1]{0:T(128)} %bitcast.1.first, bf16[6144,4096]{1,0:T(8,128)(2,1)} %all-gather.6.cloned.1.call-done.n_ref, bf16[4096,2048]{1,0:T(8,128)(2,1)} %w_ref.9), custom_call_target="tpu_custom_call" | custom-call | flops 25769803776 | bytes 35651584 | tf_op jit(solution)/shard_map/up_proj/pallas_call | solution.py:53
  204.7 18.7 %reduce-scatter.4.cloned.1.call-done = bf16[192,4096]{1,0:T(8,128)(2,1)} async-done(((bf16[1536,4096]{1,0:T(8,128)(2,1)}), bf16[192,4096]{1,0:T(8,128)(2,1)}) %reduce-scatter.4.cloned.1.call-update) | async-done | bytes 1572880 | tf_op jit(solution)/shard_map/reduce_scatter | solution.py:206
  232.3 64.6 %up_proj.5.a_ref = bf16[3072,2048]{1,0:T(8,128)(2,1)} custom-call(s32[1]{0:T(128)} %bitcast.5.first, bf16[6144,4096]{1,0:T(8,128)(2,1)} %all-gather.6.cloned.1.call-done.n_ref, bf16[4096,2048]{1,0:T(8,128)(2,1)} %w_ref.9), custom_call_target="tpu_custom_call" | custom-call | flops 51539607552 | bytes 54525952 | tf_op jit(solution)/shard_map/up_proj/pallas_call | solution.py:53
  297.2 11.4 %fusion.19.do_ref = bf16[4,1536,128]{2,1,0:T(8,128)(2,1)} fusion(bf16[4,128,4096]{2,1,0:T(8,128)(2,1)} %param.23, bf16[1536,4096]{1,0:T(8,128)(2,1)} %all-gather.8.cloned.1.call-done), kind=kOutput, calls=%fused_computation.28 | convolution fusion | flops 6443237376 | bytes 18350080 | tf_op jit(solution)/shard_map/td,hed->hte/dot_general | solution.py:221
  308.5 34.7 %attention_back.1 = (bf16[4,1536,128]{2,1,0:T(8,128)(2,1)}, bf16[3,4,1536,128]{3,2,1,0:T(8,128)(2,1)}) custom-call(bf16[3,4,1536,128]{3,2,1,0:T(8,128)(2,1)} %convert_bitcast_fusion.q_ref.k_ref.v_ref, bf16[3,4,1536,128]{3,2,1,0:T(8,128)(2,1)} %convert_bitcast_fusion.q_ref.k_ref.v_ref, bf16[3,4,1536,128]{3,2,1,0:T(8,128)(2,1)} %convert_bitcast_fusion.q_ref.k_ref.v_ref, ...), custom_call_target="tpu_custom_call" | custom-call | flops 48318382080 | bytes 12582912 | tf_op jit(solution)/shard_map/attention_back/pallas_call | solution.py:161
  343.2 14.2 %fusion.1 = f32[4,128,4096]{2,1,0:T(8,128)} fusion(bf16[4,1536,128]{2,1,0:T(8,128)(2,1)} %get-tuple-element.65, bf16[1536,4096]{1,0:T(8,128)(2,1)} %all-gather.8.cloned.1.call-done), kind=kOutput, calls=%fused_computation.8 | convolution fusion | flops 6442450944 | bytes 22544384 | tf_op jit(solution)/shard_map/hte,td->hed/dot_general | solution.py:224
  358.1 27.7 %fusion.8 = f32[3,4,128,4096]{3,2,1,0:T(8,128)} fusion(bf16[3,4,1536,128]{3,2,1,0:T(8,128)(2,1)} %get-tuple-element.57, bf16[1536,4096]{1,0:T(8,128)(2,1)} %param.13, f32[4096]{0:T(1024)S(1)} %copy-done.9, f32[1536]{0:T(1024)S(1)} %copy-done.22, f32[1536]{0:T(1024)S(1)} %copy-done.24), kind=kOutput, calls=%fused_computation.15 | convolution fusion | flops 19358810112 | bytes 42496000 | tf_op jit(solution)/shard_map/chte,td->ched/dot_general | solution.py:225
  385.8 25.5 %bitcast_convert_fusion = bf16[1536,4096]{1,0:T(8,128)(2,1)} fusion(bf16[3,4,1536,128]{3,2,1,0:T(8,128)(2,1)} %get-tuple-element.57, bf16[4096,3,4,128]{3,2,1,0:T(4,128)(2,1)} %param.22), kind=kOutput, calls=%fused_computation | convolution fusion | flops 19333644288 | bytes 29884416 | tf_op jit(solution)/shard_map/chte,dche->td/dot_general | solution.py:229
  411.3 7.0 all-to-all-start
  418.5 73.9 %all-gather.10.cloned.1.call-done.d_ref = bf16[6144,4096]{1,0:T(8,128)(2,1)} async-done(((bf16[192,4096]{1,0:T(8,128)(2,1)}), bf16[6144,4096]{1,0:T(8,128)(2,1)}) %all-gather.10.cloned.1.call-update) | async-done | bytes 50331664 | tf_op jit(solution)/shard_map/all_gather | solution.py:217
  492.3 42.5 %down_back.4 = (bf16[6144,2048]{1,0:T(8,128)(2,1)}, bf16[6144,2048]{1,0:T(8,128)(2,1)}) custom-call(s32[1]{0:T(128)} %bitcast.1.first, bf16[6144,4096]{1,0:T(8,128)(2,1)} %all-gather.10.cloned.1.call-done.d_ref, bf16[2048,4096]{1,0:T(8,128)(2,1)} %w_ref.11, bf16[1536,2048]{1,0:T(8,128)(2,1)} %up_proj.4.a_ref, ...), custom_call_target="tpu_custom_call", output_to_operand_aliasing={{0}: (4, {}), {1}: (5, {})} | custom-call | flops 25769803776 | bytes 48234496 | tf_op jit(solution)/shard_map/down_back/pallas_call | solution.py:103
  534.8 47.9 %all-to-all-done = bf16[8,192,4096]{2,1,0:T(8,128)(2,1)} async-done(((bf16[8,192,4096]{2,1,0:T(8,128)(2,1)}), bf16[8,192,4096]{2,1,0:T(8,128)(2,1)}, u32[]{:S(2)}, u32[]{:S(2)}) %all-to-all-start) | async-done | bytes 12582944 | tf_op jit(solution)/shard_map/all_to_all | solution.py:230
  582.8 7.4 convert_reduce_fusion
  592.5 5.6 add_convert_fusion
  604.6 80.1 %down_back.5 = (bf16[6144,2048]{1,0:T(8,128)(2,1)}, bf16[6144,2048]{1,0:T(8,128)(2,1)}) custom-call(s32[1]{0:T(128)} %bitcast.5.first, bf16[6144,4096]{1,0:T(8,128)(2,1)} %all-gather.10.cloned.1.call-done.d_ref, bf16[2048,4096]{1,0:T(8,128)(2,1)} %w_ref.11, bf16[3072,2048]{1,0:T(8,128)(2,1)} %up_proj.5.a_ref, ...), custom_call_target="tpu_custom_call", output_to_operand_aliasing={{0}: (4, {}), {1}: (5, {})} | custom-call | flops 51539607552 | bytes 79691776 | tf_op jit(solution)/shard_map/down_back/pallas_call | solution.py:103
  688.6 118.1 %convolution_convert_fusion.1 = bf16[2048,4096]{1,0:T(8,128)(2,1)} fusion(bf16[6144,2048]{1,0:T(8,128)(2,1)} %get-tuple-element.67, bf16[6144,4096]{1,0:T(8,128)(2,1)} %all-gather.10.cloned.1.call-done.d_ref), kind=kOutput, calls=%fused_computation.5 | convolution fusion | flops 103087603712 | bytes 92274688 | tf_op jit(solution)/shard_map/dot_general | solution.py:244
  806.7 6.4 broadcast_in_dim.2
  840.2 118.5 %convolution_convert_fusion = bf16[4096,2048]{1,0:T(8,128)(2,1)} fusion(bf16[6144,4096]{1,0:T(8,128)(2,1)} %all-gather.6.cloned.1.call-done.n_ref, bf16[6144,2048]{1,0:T(8,128)(2,1)} %get-tuple-element.79), kind=kOutput, calls=%fused_computation.4 | convolution fusion | flops 103087603712 | bytes 92274688 | tf_op jit(solution)/shard_map/dot_general | solution.py:254
  958.7 17.3 %copy.36 = bf16[4096,3,4,128]{3,2,1,0:T(4,128)(2,1)} copy(bf16[4096,3,4,128]{3,0,2,1:T(8,128)(2,1)} %bitcast.51) | data formatting | bytes 25165824
  (112 shorter events, 59.8 us)
Async XLA Ops:
  8.0 162.3 %all-gather.6.cloned.1.call-start = ((), (), s32[]{:S(2)}) async-start(), calls=%async_computation.5 | async-start | bytes 51904512 | tf_op jit(solution)/shard_map/all_gather | solution.py:200
  13.6 209.8 %reduce-scatter.4.cloned.1.call-start = ((), (), s32[]{:S(2)}) async-start(), calls=%async_computation.4 | async-start | bytes 14155776 | tf_op jit(solution)/shard_map/reduce_scatter | solution.py:206
  139.9 157.3 %all-gather.8.cloned.1.call-start = ((), (), s32[]{:S(2)}) async-start(), calls=%async_computation.6 | async-start | bytes 14155776 | tf_op jit(solution)/shard_map/all_gather | solution.py:216
  140.5 29.8 %copy-start.8 = (f32[4096]{0:T(1024)}, f32[4096]{0:T(1024)S(1)}, u32[]{:S(2)}) copy-start(f32[4096]{0:T(1024)S(1)} %convert_element_type.81) | copy-start | bytes 49156
  142.3 84.1 %copy-start = (bf16[192,4096]{1,0:T(8,128)(2,1)}, bf16[192,4096]{1,0:T(8,128)(2,1)S(1)}, u32[]{:S(2)}) copy-start(bf16[192,4096]{1,0:T(8,128)(2,1)S(1)} %constant_dynamic-slice_fusion) | copy-start | bytes 4718596
  170.3 53.1 %copy-start.6 = (f32[4096]{0:T(1024)S(1)}, f32[4096]{0:T(1024)}, u32[]{:S(2)}) copy-start(f32[4096]{0:T(1024)} %copy-done.5) | copy-start | bytes 49156
  170.3 53.1 %copy-start.11 = (f32[192]{0:T(256)S(1)}, f32[192]{0:T(256)}, u32[]{:S(2)}) copy-start(f32[192]{0:T(256)} %copy-done.10) | copy-start | bytes 2308
  170.3 53.1 %copy-start.14 = (f32[192]{0:T(256)S(1)}, f32[192]{0:T(256)}, u32[]{:S(2)}) copy-start(f32[192]{0:T(256)} %copy-done.13) | copy-start | bytes 2308
  231.5 260.8 %all-gather.10.cloned.1.call-start = ((), (), s32[]{:S(2)}) async-start(), calls=%async_computation.7 | async-start | bytes 51904512 | tf_op jit(solution)/shard_map/all_gather | solution.py:217
  232.2 452.5 %reduce-scatter.6.cloned.1.call-start = ((), (), s32[]{:S(2)}) async-start(), calls=%async_computation.8 | async-start | bytes 10485760 | tf_op jit(solution)/shard_map/reduce_scatter | solution.py:226
  357.4 458.4 %reduce-scatter.8.cloned.1.call-start = ((), (), s32[]{:S(2)}) async-start(), calls=%async_computation.9 | async-start | bytes 31457280 | tf_op jit(solution)/shard_map/reduce_scatter | solution.py:227
  411.3 171.4 %all-to-all-start = ((bf16[8,192,4096]{2,1,0:T(8,128)(2,1)}), bf16[8,192,4096]{2,1,0:T(8,128)(2,1)}, u32[]{:S(2)}, u32[]{:S(2)}) async-start(bf16[8,192,4096]{2,1,0:T(8,128)(2,1)} %bitcast.50), calls=%async_computation.1 | async-start | bytes 25165824 | tf_op jit(solution)/shard_map/all_to_all | solution.py:230
  418.3 540.3 %all-gather.14.cloned.1.call-start = ((), (), s32[]{:S(2)}) async-start(), calls=%async_computation.11 | async-start | bytes 5242880 | tf_op jit(solution)/shard_map/all_gather | solution.py:243
  598.1 89.5 %collective-permute-start = (bf16[192,4096]{1,0:T(8,128)(2,1)}, bf16[192,4096]{1,0:T(8,128)(2,1)S(1)}, u32[]{:S(2)}, u32[]{:S(2)}) collective-permute-start(bf16[192,4096]{1,0:T(8,128)(2,1)} %add_convert_fusion), channel_id=1, source_target_pairs={{0,1},{1,2},{2,3},{3,4},{4,5},{5,6},{6,7},{7,0},{8,9},{9,10},{10,1... | collective-permute-start | bytes 4718600 | tf_op jit(solution)/shard_map/ppermute | solution.py:238
  598.1 90.1 %collective-permute-start.1 = (bf16[192,4096]{1,0:T(8,128)(2,1)}, bf16[192,4096]{1,0:T(8,128)(2,1)S(1)}, u32[]{:S(2)}, u32[]{:S(2)}) collective-permute-start(bf16[192,4096]{1,0:T(8,128)(2,1)} %add_convert_fusion), channel_id=1, source_target_pairs={{0,2},{1,3},{2,4},{3,5},{4,6},{5,7},{6,0},{7,1},{8,10},{9,11},{10,... | collective-permute-start | bytes 4718600 | tf_op jit(solution)/shard_map/ppermute | solution.py:238
  598.1 217.7 %collective-permute-start.2 = (bf16[192,4096]{1,0:T(8,128)(2,1)}, bf16[192,4096]{1,0:T(8,128)(2,1)}, u32[]{:S(2)}, u32[]{:S(2)}) collective-permute-start(bf16[192,4096]{1,0:T(8,128)(2,1)} %add_convert_fusion), channel_id=1, source_target_pairs={{0,3},{1,4},{2,5},{3,6},{4,7},{5,0},{6,1},{7,2},{8,11},{9,12},{10,... | collective-permute-start | bytes 4718600 | tf_op jit(solution)/shard_map/ppermute | solution.py:238
  601.6 214.2 %collective-permute-start.3 = (bf16[192,4096]{1,0:T(8,128)(2,1)}, bf16[192,4096]{1,0:T(8,128)(2,1)}, u32[]{:S(2)}, u32[]{:S(2)}) collective-permute-start(bf16[192,4096]{1,0:T(8,128)(2,1)} %add_convert_fusion), channel_id=1, source_target_pairs={{0,4},{1,5},{2,6},{3,7},{4,0},{5,1},{6,2},{7,3},{8,12},{9,13},{10,... | collective-permute-start | bytes 4718600 | tf_op jit(solution)/shard_map/ppermute | solution.py:238
  601.9 213.9 %collective-permute-start.4 = (bf16[192,4096]{1,0:T(8,128)(2,1)}, bf16[192,4096]{1,0:T(8,128)(2,1)}, u32[]{:S(2)}, u32[]{:S(2)}) collective-permute-start(bf16[192,4096]{1,0:T(8,128)(2,1)} %add_convert_fusion), channel_id=1, source_target_pairs={{0,5},{1,6},{2,7},{3,0},{4,1},{5,2},{6,3},{7,4},{8,13},{9,14},{10,... | collective-permute-start | bytes 4718600 | tf_op jit(solution)/shard_map/ppermute | solution.py:238
  687.5 271.1 %all-gather.12.cloned.1.call-start = ((), (), s32[]{:S(2)}) async-start(), calls=%async_computation.10 | async-start | bytes 15728640 | tf_op jit(solution)/shard_map/all_gather | solution.py:252
  687.6 119.1 %copy-start.2 = (bf16[192,4096]{1,0:T(8,128)(2,1)}, bf16[192,4096]{1,0:T(8,128)(2,1)S(1)}, u32[]{:S(2)}) copy-start(bf16[192,4096]{1,0:T(8,128)(2,1)S(1)} %collective-permute-done) | copy-start | bytes 4718596
  687.6 128.2 %collective-permute-start.5 = (bf16[192,4096]{1,0:T(8,128)(2,1)}, bf16[192,4096]{1,0:T(8,128)(2,1)}, u32[]{:S(2)}, u32[]{:S(2)}) collective-permute-start(bf16[192,4096]{1,0:T(8,128)(2,1)} %add_convert_fusion), channel_id=1, source_target_pairs={{0,6},{1,7},{2,0},{3,1},{4,2},{5,3},{6,4},{7,5},{8,14},{9,15},{10,... | collective-permute-start | bytes 4718600 | tf_op jit(solution)/shard_map/ppermute | solution.py:238
  688.2 118.5 %copy-start.3 = (bf16[192,4096]{1,0:T(8,128)(2,1)}, bf16[192,4096]{1,0:T(8,128)(2,1)S(1)}, u32[]{:S(2)}) copy-start(bf16[192,4096]{1,0:T(8,128)(2,1)S(1)} %collective-permute-done.1) | copy-start | bytes 4718596
  688.2 127.6 %collective-permute-start.6 = (bf16[192,4096]{1,0:T(8,128)(2,1)}, bf16[192,4096]{1,0:T(8,128)(2,1)}, u32[]{:S(2)}, u32[]{:S(2)}) collective-permute-start(bf16[192,4096]{1,0:T(8,128)(2,1)} %add_convert_fusion), channel_id=1, source_target_pairs={{0,7},{1,0},{2,1},{3,2},{4,3},{5,4},{6,5},{7,6},{8,15},{9,8},{10,9... | collective-permute-start | bytes 4718600 | tf_op jit(solution)/shard_map/ppermute | solution.py:238
  958.6 17.3 %copy-start.1 = (bf16[512,4096]{1,0:T(8,128)(2,1)S(1)}, bf16[512,4096]{1,0:T(8,128)(2,1)}, u32[]{:S(2)}) copy-start(bf16[512,4096]{1,0:T(8,128)(2,1)} %all-gather.14.cloned.1.call-done) | copy-start | bytes 12582916
  (17 other events, 79.3 us)
Sparse Core Ops, SparseCore 0:
  13.7 155.3 all-gather.5
  357.5 159.7 reduce-scatter.5
  519.7 212.8 reduce-scatter.7
  734.0 45.3 all-gather.13
  822.0 116.8 all-gather.11
Sparse Core Ops, SparseCore 1:
  139.9 83.5 reduce-scatter.3
  231.6 65.5 all-gather.7
  299.1 193.2 all-gather.9
